TPU v7x, 32 devices: a whole 2x2x4 slice. The times are simulated.
32 devices in a mesh: row: 8 (over z, y), col: 2 (over core), depth: 2 (over x).
Axes of the slice: x: 2, y: 2, z: 4, core: 2. Of those that a mesh axis runs over, the one named last changes fastest.
Arguments:
- student_hidden: bfloat16 [2048, 768], P('row', ('depth', 'col')), may hold values from -16 to 16
- embedding: bfloat16 [50304, 768], P('col', ('depth', 'row')), as said below
- teacher_logits: bfloat16 [2048, 50304], P('row', ('col', 'depth')), may hold values from -24 to 124, as said below
Outputs:
- loss: float32 [2048], P('row')
- peak_logprob: float32 [2048], P('row')
Inputs may be any that keep to these rules, and one draw needn't show every extreme that they name: embedding entries lie within plus or minus 4 / sqrt(768). teacher_logits lie within -24 and 124; each token's logits carry an offset of 0 to 100.
All inputs are finite; a program needn't handle non-finite values.
Results may differ from a plain program's by a relative error of at most 0.0003.
Values may be sent and summed in bfloat16 or wider, within the bound.
A program may use at most 128 MiB of HBM per device.

v0:
```python
import jax
import jax.numpy as jnp
from jax import lax
from jax.sharding import PartitionSpec as P


def row_terms(student, teacher_values, student_peak, teacher_peak):
    weights = jnp.exp(teacher_values - teacher_peak[:, None])
    student_sum = jnp.sum(jnp.exp(student - student_peak[:, None]), axis=1)
    teacher_sum = jnp.sum(weights, axis=1)
    cross_sum = jnp.sum(weights * student, axis=1)
    return (student_sum, teacher_sum, cross_sum)


def on_device(student_hidden, embedding, teacher_logits):
    hidden_layer = lax.all_gather(student_hidden, "col", axis=1, tiled=True)
    token_count = hidden_layer.shape[0]
    hidden_full = lax.all_gather(hidden_layer, "depth", axis=1, tiled=True)
    row_count = lax.axis_size("row")
    depth_count = lax.axis_size("depth")
    narrow = embedding.shape[1]
    hidden_order = hidden_full.reshape(token_count, depth_count, row_count, narrow)
    hidden_order = hidden_order.transpose(0, 2, 1, 3).reshape(
        token_count, row_count * depth_count * narrow
    )
    vocab_rows = lax.all_to_all(embedding, "depth", split_axis=0, concat_axis=1, tiled=True)
    full_rows = lax.all_gather(vocab_rows, "row", axis=1, tiled=True)
    student = jnp.einsum("td,vd->tv", hidden_order, full_rows, preferred_element_type=jnp.float32)
    teacher_values = teacher_logits.astype(jnp.float32)
    student_top = jnp.max(student, axis=1)
    teacher_top = jnp.max(teacher_values, axis=1)
    student_peak, teacher_peak = lax.pmax((student_top, teacher_top), ("col", "depth"))
    local_student, local_teacher, local_cross = row_terms(
        student, teacher_values, student_peak, teacher_peak
    )
    student_sum, teacher_sum, cross_sum = lax.psum(
        (local_student, local_teacher, local_cross), ("col", "depth")
    )
    norm_log = jnp.log(student_sum)
    loss = student_peak + norm_log - cross_sum / teacher_sum
    return (loss, -norm_log)


def solution(mesh):
    in_specs = (P("row", ("depth", "col")), P("col", ("depth", "row")), P("row", ("col", "depth")))
    out_specs = (P("row"), P("row"))
    return jax.shard_map(
        on_device, mesh=mesh, in_specs=in_specs, out_specs=out_specs, check_vma=False
    )
```

profile of v0, /device:TPU:0, one launch (start us, length us, event | category | flops | bytes accessed | tf_op | source)
XLA Modules:
  0.0 464.3 jit_solution(10611060444776623536)
XLA Ops:
  7.2 0.0 copy-start
  7.2 0.0 all-gather.2.cloned.1.call-start
  7.2 3.9 all_to_all.14
  11.1 0.2 copy.8
  11.4 33.4 %all_to_all.19 = bf16[2,12576,48]{1,2,0:T(8,128)(2,1)} all-to-all(bf16[2,12576,48]{1,2,0:T(8,128)(2,1)S(1)} %copy.8), channel_id=1, replica_groups=mesh['row'=8,'col'=2,'depth'=2] {'depth'}, dimensions={0} | all-to-all | bytes 4829184 | tf_op jit(solution)/shard_map/all_to_all | solution.py:26
  44.8 0.0 all-gather.2.cloned.1.call-update
  44.8 0.0 copy-done
  44.8 1.9 all_gather.9
  46.8 7.6 %all_gather.10 = bf16[256,768]{0,1:T(8,128)(2,1)S(1)} all-gather(bf16[256,384]{0,1:T(8,128)(2,1)S(1)} %all_gather.9), channel_id=1, replica_groups=mesh['row'=8,'col'=2,'depth'=2] {'depth'}, dimensions={1}, use_global_device_ids=true | all-gather | bytes 589824 | tf_op jit(solution)/shard_map/all_gather | solution.py:18
  54.4 4.4 reduce_max.24
  58.8 360.2 %all-gather.2.cloned.1.call-done = bf16[12576,768]{0,1:T(8,128)(2,1)} async-done(((bf16[12576,96]{0,1:T(8,128)(2,1)}), bf16[12576,768]{0,1:T(8,128)(2,1)}) %all-gather.2.cloned.1.call-update) | async-done | bytes 19316752 | tf_op jit(solution)/shard_map/all_gather | solution.py:27
  419.0 14.5 %fusion.1 = (f32[256]{0:T(256)S(1)}, f32[256,12576]{0,1:T(8,128)}) fusion(bf16[256,768]{0,1:T(8,128)(2,1)S(1)} %bitcast.12, bf16[12576,768]{0,1:T(8,128)(2,1)} %all-gather.2.cloned.1.call-done), kind=kOutput, calls=%fused_computation.6 | convolution fusion | flops 4948303872 | bytes 32588800 | tf_op jit(solution)/shard_map/td,vd->tv/dot_general | solution.py:28
  433.5 7.4 %all-reduce.1 = (f32[256]{0:T(256)S(1)}, f32[256]{0:T(256)S(1)}) all-reduce(f32[256]{0:T(256)S(1)} %get-tuple-element.12, bf16[256]{0:T(256)(128)(2,1)S(1)} %reduce_max.24), channel_id=1, replica_groups=mesh['row'=8,'col'=2,'depth'=2] {'col','depth'}, use_global_device_ids=true, to_apply=%region_1.0 | all-reduce | flops 512 | bytes 3584 | tf_op jit(solution)/shard_map/pmax | solution.py:32
  440.9 8.9 %exponential_reduce_fusion = (f32[256]{0:T(256)S(1)}, f32[256]{0:T(256)S(1)}, f32[256]{0:T(256)S(1)}) fusion(f32[256,12576]{0,1:T(8,128)} %get-tuple-element.13, f32[256]{0:T(256)S(1)} %get-tuple-element.8, f32[256]{0:T(256)S(1)} %get-tuple-element.9, bf16[256,12576]{0,1:T(8,128)(2,1)} %param.5), kind=kLoop, calls=%fused_computation.3 | loop fusion | flops 22535424 | bytes 19321856 | tf_op jit(solution)/shard_map/reduce_sum | solution.py:9
  449.8 7.1 %all-reduce = (f32[256]{0:T(256)S(1)}, f32[256]{0:T(256)S(1)}, f32[256]{0:T(256)S(1)}) all-reduce(f32[256]{0:T(256)S(1)} %get-tuple-element.3, f32[256]{0:T(256)S(1)} %get-tuple-element.4, f32[256]{0:T(256)S(1)} %get-tuple-element.2), channel_id=1, replica_groups=mesh['row'=8,'col'=2,'depth'=2] {'col','depth'}, use_global_device_ids=true, to_apply=%region_7.0 | all-reduce | flops 768 | bytes 6144 | tf_op jit(solution)/shard_map/psum | solution.py:36
  456.9 0.6 log_negate_fusion
  (1 shorter events, 0.0 us)
Async XLA Ops:
  7.2 37.7 %copy-start = (bf16[256,192]{0,1:T(8,128)(2,1)S(1)}, bf16[256,192]{0,1:T(8,128)(2,1)}, u32[]{:S(2)}) copy-start(bf16[256,192]{0,1:T(8,128)(2,1)} %param.3) | copy-start | bytes 294916
  7.2 411.8 %all-gather.2.cloned.1.call-start = ((), (), s32[]{:S(2)}) async-start(), calls=%async_computation.1 | async-start | bytes 21897216 | tf_op jit(solution)/shard_map/all_gather | solution.py:27
Sparse Core Ops, SparseCore 0:
  44.9 374.0 all-gather.1
where the time goes:
time: 465 us; the launch traced here: 464 us
  waiting for transfers between devices  360 us (77%)
  blocking collectives  57.5 us (12%)
  matrix products  14.5 us (3%)
  between operations  14.1 us (3%)
  other arithmetic  13.8 us (3%)
    all_gather x1, waiting for transfers between devices, on_device(): full_rows = lax.all_gather(vocab_rows, 'row', axis=1, tiled=True)  360 us
    all_to_all x1, blocking collectives, on_device(): lax.all_to_all(embedding, 'depth', split_axis=0, concat_axis=1, tiled=True)  33.4 us
    dot_general x1, matrix products, on_device(): jnp.einsum('td,vd->tv', hidden_order, full_rows, preferred_element_type=j...  14.5 us
  transfers between devices with their start and end apart: 1, of which 1 were waited for; matrix products, arithmetic and copies ran while one was open for 1% of the time, Pallas kernels for 0%

commit v1 on v0

--- a/solution.py
+++ b/solution.py
@@ -1,7 +1,21 @@
+import functools
 import jax
 import jax.numpy as jnp
 from jax import lax
 from jax.sharding import PartitionSpec as P
+from jax.lax import all_to_all, axis_size
+
+
+def bind_frames_by_axis(chunk, comm_axis, where_dim):
+    sides = []
+    for _ in range(axis_size(comm_axis)):
+        sides.append(chunk)
+    later = jnp.stack(sides, axis=0)
+    x_now = jnp.concatenate(all_to_all(later, comm_axis, 0, 0), where_dim)
+    return x_now
+
+
+draw_values_up = functools.partial(bind_frames_by_axis, comm_axis="row", where_dim=1)
 
 
 def row_terms(student, teacher_values, student_peak, teacher_peak):
@@ -24,7 +38,7 @@
         token_count, row_count * depth_count * narrow
     )
     vocab_rows = lax.all_to_all(embedding, "depth", split_axis=0, concat_axis=1, tiled=True)
-    full_rows = lax.all_gather(vocab_rows, "row", axis=1, tiled=True)
+    full_rows = draw_values_up(vocab_rows)
     student = jnp.einsum("td,vd->tv", hidden_order, full_rows, preferred_element_type=jnp.float32)
     teacher_values = teacher_logits.astype(jnp.float32)
     student_top = jnp.max(student, axis=1)

time: 465 us -> 509 us (1.095)
  waiting for transfers between devices: 360 us -> 406 us
  between operations: 14.1 us -> 0.66 us
  local copies, waits for them, and re-layouts: 4.17 us -> 11.1 us
  starting transfers between devices: 0.04 us -> 6.21 us
    all_to_all x0 -> x1, waiting for transfers between devices: none -> 406 us  [bind_frames_by_axis(): x_now = jnp.concatenate(all_to_all(later, comm_axis, 0, 0), where_dim)]
    all_gather x1 -> x0, waiting for transfers between devices: 360 us -> none  [on_device(): full_rows = lax.all_gather(vocab_rows, 'row', axis=1, tiled=True)]
    another operation x0 -> x1, local copies, waits for them, and re-layouts: none -> 6.95 us  [bind_frames_by_axis(): later = jnp.stack(sides, axis=0)]
    all_to_all x0 -> x1, starting transfers between devices: none -> 6.21 us  [bind_frames_by_axis(): x_now = jnp.concatenate(all_to_all(later, comm_axis, 0, 0), where_dim)]
where the time goes in v1:
time: 509 us
  waiting for transfers between devices  406 us (80%)
  blocking collectives  56.5 us (11%)
  matrix products  14.5 us (3%)
  other arithmetic  13.8 us (3%)
  local copies, waits for them, and re-layouts  11.1 us (2%)
  starting transfers between devices  6.21 us (1%)
    all_to_all x1, waiting for transfers between devices, bind_frames_by_axis(): x_now = jnp.concatenate(all_to_all(later, comm_axis, 0, 0), where_dim)  406 us
    all_to_all x1, blocking collectives, on_device(): lax.all_to_all(embedding, 'depth', split_axis=0, concat_axis=1, tiled=True)  32.5 us
    dot_general x1, matrix products, on_device(): jnp.einsum('td,vd->tv', hidden_order, full_rows, preferred_element_type=j...  14.5 us
  transfers between devices with their start and end apart: 1, of which 1 were waited for; matrix products, arithmetic and copies ran while one was open for 1% of the time, Pallas kernels for 0%

profile of v1, /device:TPU:0, one launch (start us, length us, event | category | flops | bytes accessed | tf_op | source)
XLA Modules:
  0.0 508.9 jit_solution(8812044764522152691)
XLA Ops:
  0.6 3.9 all_to_all.15
  4.5 0.2 copy.8
  4.8 32.5 %all_to_all.21 = bf16[2,12576,48]{1,2,0:T(8,128)(2,1)S(1)} all-to-all(bf16[2,12576,48]{1,2,0:T(8,128)(2,1)S(1)} %copy.8), channel_id=1, replica_groups=mesh['row'=8,'col'=2,'depth'=2] {'depth'}, dimensions={0} | all-to-all | bytes 4829184 | tf_op jit(solution)/shard_map/all_to_all | solution.py:40
  37.3 6.9 %stack.5 = bf16[8,12576,96]{1,2,0:T(8,128)(2,1)} broadcast(bf16[12576,96]{0,1:T(8,128)(2,1)S(1)} %bitcast.14), dimensions={1,2} | broadcast | bytes 21731328 | tf_op jit(solution)/shard_map/stack | solution.py:13
  44.2 0.0 copy-start
  44.2 6.2 %all-to-all-start.1 = ((bf16[8,12576,96]{1,2,0:T(8,128)(2,1)}), bf16[8,12576,96]{1,2,0:T(8,128)(2,1)}, u32[]{:S(2)}, u32[]{:S(2)}) async-start(bf16[8,12576,96]{1,2,0:T(8,128)(2,1)} %stack.5), calls=%async_computation.1 | async-start | bytes 38928384 | tf_op jit(solution)/shard_map/all_to_all | solution.py:14
  50.4 0.0 copy-done
  50.4 1.9 all_gather.6
  52.4 7.6 %all_gather.7 = bf16[256,768]{0,1:T(8,128)(2,1)S(1)} all-gather(bf16[256,384]{0,1:T(8,128)(2,1)S(1)} %all_gather.6), channel_id=1, replica_groups=mesh['row'=8,'col'=2,'depth'=2] {'depth'}, dimensions={1}, use_global_device_ids=true | all-gather | bytes 589824 | tf_op jit(solution)/shard_map/all_gather | solution.py:32
  60.0 4.4 reduce_max.24
  64.4 406.1 %all-to-all-done.1 = bf16[8,12576,96]{1,2,0:T(8,128)(2,1)} async-done(((bf16[8,12576,96]{1,2,0:T(8,128)(2,1)}), bf16[8,12576,96]{1,2,0:T(8,128)(2,1)}, u32[]{:S(2)}, u32[]{:S(2)}) %all-to-all-start.1) | async-done | bytes 19316768 | tf_op jit(solution)/shard_map/all_to_all | solution.py:14
  470.5 14.5 %fusion.1 = (f32[256]{0:T(256)S(1)}, f32[256,12576]{0,1:T(8,128)}) fusion(bf16[256,768]{0,1:T(8,128)(2,1)S(1)} %bitcast.15, bf16[12576,768]{0,1:T(8,128)(2,1)} %bitcast.6), kind=kOutput, calls=%fused_computation.6 | convolution fusion | flops 4948303872 | bytes 32588800 | tf_op jit(solution)/shard_map/td,vd->tv/dot_general | solution.py:42
  485.0 6.5 %all-reduce.1 = (f32[256]{0:T(256)S(1)}, f32[256]{0:T(256)S(1)}) all-reduce(f32[256]{0:T(256)S(1)} %get-tuple-element.12, bf16[256]{0:T(256)(128)(2,1)S(1)} %reduce_max.24), channel_id=1, replica_groups=mesh['row'=8,'col'=2,'depth'=2] {'col','depth'}, use_global_device_ids=true, to_apply=%region_1.0 | all-reduce | flops 512 | bytes 3584 | tf_op jit(solution)/shard_map/pmax | solution.py:46
  491.5 8.9 %exponential_reduce_fusion = (f32[256]{0:T(256)S(1)}, f32[256]{0:T(256)S(1)}, f32[256]{0:T(256)S(1)}) fusion(f32[256,12576]{0,1:T(8,128)} %get-tuple-element.13, f32[256]{0:T(256)S(1)} %get-tuple-element.8, f32[256]{0:T(256)S(1)} %get-tuple-element.9, bf16[256,12576]{0,1:T(8,128)(2,1)} %param.5), kind=kLoop, calls=%fused_computation.3 | loop fusion | flops 22535424 | bytes 19321856 | tf_op jit(solution)/shard_map/reduce_sum | solution.py:23
  500.4 8.0 %all-reduce = (f32[256]{0:T(256)S(1)}, f32[256]{0:T(256)S(1)}, f32[256]{0:T(256)S(1)}) all-reduce(f32[256]{0:T(256)S(1)} %get-tuple-element.3, f32[256]{0:T(256)S(1)} %get-tuple-element.4, f32[256]{0:T(256)S(1)} %get-tuple-element.2), channel_id=1, replica_groups=mesh['row'=8,'col'=2,'depth'=2] {'col','depth'}, use_global_device_ids=true, to_apply=%region_7.0 | all-reduce | flops 768 | bytes 6144 | tf_op jit(solution)/shard_map/psum | solution.py:50
  508.4 0.6 log_negate_fusion
  (1 shorter events, 0.0 us)
Async XLA Ops:
  44.2 6.2 %copy-start = (bf16[256,192]{0,1:T(8,128)(2,1)S(1)}, bf16[256,192]{0,1:T(8,128)(2,1)}, u32[]{:S(2)}) copy-start(bf16[256,192]{0,1:T(8,128)(2,1)} %param.3) | copy-start | bytes 294916
  44.2 426.3 %all-to-all-start.1 = ((bf16[8,12576,96]{1,2,0:T(8,128)(2,1)}), bf16[8,12576,96]{1,2,0:T(8,128)(2,1)}, u32[]{:S(2)}, u32[]{:S(2)}) async-start(bf16[8,12576,96]{1,2,0:T(8,128)(2,1)} %stack.5), calls=%async_computation.1 | async-start | bytes 38928384 | tf_op jit(solution)/shard_map/all_to_all | solution.py:14
